TPU v7x, 32 devices: a whole 2x2x4 slice. The times are simulated.
32 devices in a mesh: limb: 4 (over z), coef: 8 (over y, x, core).
Axes of the slice: x: 2, y: 2, z: 4, core: 2. Of those that a mesh axis runs over, the one named last changes fastest.
Arguments:
- cipher_zero: float32 [24, 32, 65536], P(None, 'limb', 'coef'), may hold values from -6 to 6
- cipher_one: float32 [24, 32, 65536], P(None, 'limb', 'coef'), may hold values from -6 to 6
- key_main: bfloat16 [24, 2, 2, 32, 65536], P(None, None, None, 'limb', 'coef'), may hold values from -5 to 5
- key_special: bfloat16 [24, 2, 2, 16, 65536], P(None, None, None, 'limb', 'coef'), may hold values from -5 to 5
- lift_main: float32 [32, 32], replicated, may hold values from -1.5 to 1.5
- lift_special: float32 [32, 16], replicated, may hold values from -1.5 to 1.5
- lower_table: float32 [16, 32], replicated, may hold values from -1.5 to 1.5
- inverse_scale: float32 [32], P('limb'), may hold values from 0.5 to 1.5
- inverse_main: float32 [32, 256, 256], P('limb', 'coef'), may hold values from 0.5 to 1.5
- inverse_special: float32 [16, 256, 256], P('limb', 'coef'), may hold values from 0.5 to 1.5
- forward_main: float32 [32, 256, 256], P('limb', 'coef'), may hold values from 0.5 to 1.5
- forward_special: float32 [16, 256, 256], P('limb', 'coef'), may hold values from 0.5 to 1.5
- inverse_rows: float32 [256, 256], replicated, may hold values from -0.375 to 0.375
- inverse_columns: float32 [256, 256], replicated, may hold values from -0.375 to 0.375
- forward_rows: float32 [256, 256], replicated, may hold values from -0.375 to 0.375
- forward_columns: float32 [256, 256], replicated, may hold values from -0.375 to 0.375
Outputs:
- switched_zero: float32 [24, 32, 65536], P(None, 'limb', 'coef')
- switched_one: float32 [24, 32, 65536], P(None, 'limb', 'coef')
All inputs are finite; a program needn't handle non-finite values.
Results may differ from a plain program's by a relative error of at most 0.0003.
Values sent between devices are 32-bit elements; how exact they have to be, the bound alone decides.
No kernel may reach another device: no remote copies, remote signals or barrier semaphores. Data moves between devices by JAX's collectives and lax.ppermute only.
A program may use at most 192 MiB of HBM per device.

v0:
```python
import jax
import jax.numpy as jnp
from jax import lax
from jax.sharding import PartitionSpec as P

K = 16
ROWS = 256
COLS = 256
HIGHEST = lax.Precision.HIGHEST


def columns_section(values, twiddle, inverse_columns):
    partial_value = (
        jnp.einsum("...rc,ck->...rk", values, inverse_columns, precision=HIGHEST) * twiddle
    )
    flattened = partial_value.reshape((-1,) + partial_value.shape[-2:])
    return lax.all_to_all(flattened, "coef", split_axis=2, concat_axis=1, tiled=True)


def to_coefficients(values, twiddle, inverse_rows, inverse_columns):
    leading = values.shape[:-2]
    arrived = columns_section(values, twiddle, inverse_columns)
    output = jnp.einsum("brk,rj->bkj", arrived, inverse_rows, precision=HIGHEST)
    return output.reshape(leading + output.shape[-2:])


def to_values(coeffs, twiddle, forward_rows, forward_columns):
    leading = coeffs.shape[:-2]
    partial_value = jnp.einsum("...cr,rk->...ck", coeffs, forward_rows, precision=HIGHEST) * twiddle
    flattened = partial_value.reshape((-1,) + partial_value.shape[-2:])
    arrived = lax.all_to_all(flattened, "coef", split_axis=2, concat_axis=1, tiled=True)
    output = jnp.einsum("bck,cm->bkm", arrived, forward_columns, precision=HIGHEST)
    return output.reshape(leading + output.shape[-2:])


def on_device(
    cipher_zero,
    cipher_one,
    key_main,
    key_special,
    lift_main,
    lift_special,
    lower_table,
    inverse_scale,
    inverse_main,
    inverse_special,
    forward_main,
    forward_special,
    inverse_rows,
    inverse_columns,
    forward_rows,
    forward_columns,
):
    ciphers, local_main, positions = cipher_one.shape
    local_special = key_special.shape[3]
    digits = key_main.shape[1]
    rows_here = inverse_main.shape[1]
    cols_here = forward_main.shape[1]
    total_main = lift_main.shape[0]
    limb_index = lax.axis_index("limb")
    owner = (jnp.arange(total_main) // K)[None, :] == jnp.arange(digits)[:, None]
    digit_mask = owner.astype(lift_main.dtype)
    masked_main = digit_mask[:, :, None] * lift_main[None]
    masked_special = digit_mask[:, :, None] * lift_special[None]
    twiddle_both = jnp.concatenate([forward_main, forward_special], axis=0)
    shaped = cipher_one.reshape(ciphers, local_main, rows_here, COLS)
    coeffs = to_coefficients(shaped, inverse_main, inverse_rows, inverse_columns).reshape(
        ciphers, local_main, positions
    )
    own_main = lax.dynamic_slice_in_dim(masked_main, limb_index * local_main, local_main, 2)
    own_special = lax.dynamic_slice_in_dim(
        masked_special, limb_index * local_special, local_special, 2
    )
    portion = lax.all_gather(coeffs, "limb", axis=1, tiled=True)
    lifted_main = jnp.einsum("bsn,dst->bdtn", portion, own_main, precision=HIGHEST)
    lifted_sp = jnp.einsum("bsn,dst->bdtn", portion, own_special, precision=HIGHEST)
    joined = jnp.concatenate([lifted_main, lifted_sp], axis=2)
    joined = joined.reshape(ciphers, digits, local_main + local_special, cols_here, ROWS)
    values_all = to_values(joined, twiddle_both, forward_rows, forward_columns)
    values_all = values_all.reshape(ciphers, digits, local_main + local_special, positions)
    values_main = values_all[:, :, :local_main]
    values_sp = values_all[:, :, local_main:]
    summed_main = jnp.sum(values_main[:, :, None] * key_main.astype(jnp.float32), axis=1)
    summed_sp = jnp.sum(values_sp[:, :, None] * key_special.astype(jnp.float32), axis=1)
    shaped_sp = summed_sp.reshape(ciphers, 2, local_special, rows_here, COLS)
    special = to_coefficients(shaped_sp, inverse_special, inverse_rows, inverse_columns)
    special = special.reshape(ciphers, 2, local_special, positions)
    own_lower = lax.dynamic_slice_in_dim(lower_table, limb_index * local_main, local_main, 1)
    lowered = jnp.einsum(
        "bsjn,jt->bstn",
        lax.all_gather(special, "limb", axis=2, tiled=True),
        own_lower,
        precision=HIGHEST,
    )
    lowered = to_values(
        lowered.reshape(ciphers, 2, local_main, cols_here, ROWS),
        forward_main,
        forward_rows,
        forward_columns,
    )
    lowered = lowered.reshape(ciphers, 2, local_main, positions)
    result = inverse_scale[:, None] * (summed_main - lowered)
    return (cipher_zero + result[:, 0], result[:, 1])


def solution(mesh):
    placed = (
        P(None, "limb", "coef"),
        P(None, "limb", "coef"),
        P(None, None, None, "limb", "coef"),
        P(None, None, None, "limb", "coef"),
        P(),
        P(),
        P(),
        P("limb"),
        P("limb", "coef", None),
        P("limb", "coef", None),
        P("limb", "coef", None),
        P("limb", "coef", None),
        P(),
        P(),
        P(),
        P(),
    )
    return jax.shard_map(
        on_device,
        mesh=mesh,
        in_specs=placed,
        out_specs=(P(None, "limb", "coef"), P(None, "limb", "coef")),
        check_vma=False,
    )
```

profile of v0, /device:TPU:0, one launch (start us, length us, event | category | flops | bytes accessed | tf_op | source)
XLA Modules:
  0.0 1902.5 jit_solution(8218457899947715766)
XLA Ops:
  7.2 0.0 copy-start
  7.2 0.0 all-gather.3.cloned.1.call-start
  7.2 10.8 broadcast_multiply_fusion.3
  18.0 9.6 copy.48
  27.6 99.7 %all_to_all.72 = f32[192,32,256]{0,1,2:T(8,128)S(1)} all-to-all(f32[192,32,256]{0,1,2:T(8,128)} %copy.48), channel_id=1, replica_groups=mesh['limb'=4,'coef'=8] {'coef'}, dimensions={2} | all-to-all | bytes 12582912 | tf_op jit(solution)/shard_map/all_to_all | solution.py:17
  127.3 8.0 copy.50
  135.2 9.7 copy.51
  145.0 0.0 copy-done.7
  145.0 8.8 fusion.35
  153.8 7.2 reshape_reshape.12
  161.0 0.0 all-gather.3.cloned.1.call-update
  161.0 0.2 all-gather.5.cloned.1.call-start
  161.3 0.1 copy.46
  161.3 0.7 constant_dynamic-slice_fusion
  162.1 0.0 copy-done.10
  162.1 0.6 compare_convert_fusion
  162.7 423.1 %all-gather.3.cloned.1.call-done = f32[24,32,8192]{2,1,0:T(8,128)} async-done(((f32[24,8,8192]{2,1,0:T(8,128)}), f32[24,32,8192]{2,1,0:T(8,128)}) %all-gather.3.cloned.1.call-update) | async-done | bytes 25165840 | tf_op jit(solution)/shard_map/all_gather | solution.py:74
  585.8 16.9 fusion.13
  602.7 0.0 copy-done.1
  602.7 15.7 fusion.10
  618.5 14.2 pad_maximum_fusion
  632.7 21.5 %reshape.87 = f32[24,2,12,32,256]{4,3,2,0,1:T(8,128)} reshape(f32[24,2,12,8192]{3,2,0,1:T(8,128)} %pad_maximum_fusion) | data formatting | bytes 37748736 | tf_op jit(solution)/shard_map/reshape | solution.py:78
  654.2 0.0 copy-done
  654.2 20.6 %broadcast_multiply_fusion = f32[24,2,12,32,256]{4,3,2,1,0:T(8,128)} fusion(f32[12,32,256]{2,1,0:T(8,128)S(1)} %pad_maximum_fusion.1, f32[24,2,12,32,256]{4,3,2,0,1:T(8,128)} %reshape.87, f32[256,256]{1,0:T(8,128)S(1)} %copy-done), kind=kOutput, calls=%fused_computation.16 | convolution fusion | flops 14500233216 | bytes 38404096 | tf_op jit(solution)/shard_map/...cr,rk->...ck/dot_general | solution.py:29
  674.8 23.4 %copy.54 = f32[576,32,256]{0,1,2:T(8,128)} copy(f32[576,32,256]{2,1,0:T(8,128)} %bitcast.95) | data formatting | bytes 37748736 | tf_op jit(solution)/shard_map/reshape | solution.py:30
  698.2 233.5 %all_to_all.73 = f32[576,32,256]{0,1,2:T(8,128)S(1)} all-to-all(f32[576,32,256]{0,1,2:T(8,128)} %copy.54), channel_id=1, replica_groups=mesh['limb'=4,'coef'=8] {'coef'}, dimensions={2} | all-to-all | bytes 37748736 | tf_op jit(solution)/shard_map/all_to_all | solution.py:31
  931.8 14.1 copy.56
  945.9 21.5 %copy.57 = f32[576,256,32]{1,2,0:T(8,128)} copy(f32[576,256,32]{0,2,1:T(8,128)} %bitcast.97) | data formatting | bytes 37748736 | tf_op jit(solution)/shard_map/all_to_all | solution.py:31
  967.4 0.0 copy-done.2
  967.4 20.2 %fusion.31 = f32[576,32,256]{2,1,0:T(8,128)} fusion(f32[576,256,32]{1,2,0:T(8,128)} %copy.57, f32[256,256]{1,0:T(8,128)S(1)} %copy-done.2), kind=kOutput, calls=%fused_computation.32 | convolution fusion | flops 14495514624 | bytes 38010880 | tf_op jit(solution)/shard_map/bck,cm->bkm/dot_general | solution.py:32
  987.6 20.6 %reshape_reshape.13 = f32[24,2,12,8192]{3,2,1,0:T(8,128)} reshape(f32[576,32,256]{2,1,0:T(8,128)} %fusion.31) | data formatting | bytes 37748736 | tf_op jit(solution)/shard_map/reshape;reshape | solution.py:80
  1008.1 5.5 slice.17
  1013.7 0.0 copy-start.9
  1013.7 11.3 multiply_reduce_fusion.1
  1025.0 8.5 reshape.74
  1033.5 0.0 copy-done.9
  1033.5 9.1 broadcast_multiply_fusion.2
  1042.6 9.6 copy.59
  1052.2 97.8 %all_to_all.74 = f32[192,32,256]{0,1,2:T(8,128)S(1)} all-to-all(f32[192,32,256]{0,1,2:T(8,128)} %copy.59), channel_id=1, replica_groups=mesh['limb'=4,'coef'=8] {'coef'}, dimensions={2} | all-to-all | bytes 12582912 | tf_op jit(solution)/shard_map/all_to_all | solution.py:17
  1149.9 8.0 copy.61
  1157.9 9.7 copy.62
  1167.6 8.8 fusion.33
  1176.5 8.6 reshape_reshape.14
  1185.1 0.0 copy-start.12
  1185.1 9.1 copy.63
  1194.2 0.0 all-gather.5.cloned.1.call-update
  1194.2 0.0 copy-start.5
  1194.3 421.7 %all-gather.5.cloned.1.call-done = f32[24,2,16,8192]{3,0,1,2:T(8,128)} async-done(((f32[24,2,4,8192]{3,0,1,2:T(8,128)}), f32[24,2,16,8192]{3,0,1,2:T(8,128)}) %all-gather.5.cloned.1.call-update) | async-done | bytes 25165840 | tf_op jit(solution)/shard_map/all_gather | solution.py:91
  1615.9 0.0 copy-done.12
  1615.9 34.7 %fusion.4 = f32[8,24,2,8192]{3,0,2,1:T(8,128)S(1)} fusion(f32[24,2,16,8192]{3,0,1,2:T(8,128)} %all-gather.5.cloned.1.call-done, f32[16,32]{1,0:T(8,128)S(1)} %copy-done.12, s32[]{:T(128)S(6)} %select_n.19), kind=kOutput, calls=%fused_computation.5 | convolution fusion | flops 603979776 | bytes 37750788 | tf_op jit(solution)/shard_map/bsjn,jt->bstn/dot_general | solution.py:89
  1650.7 13.7 broadcast_multiply_fusion.1
  1664.4 12.9 copy.66
  1677.2 5.4 all-to-all-start.3
  1682.6 10.4 slice.16
  1693.1 15.5 multiply_reduce_fusion
  1708.6 113.0 %all-to-all-done.3 = f32[384,32,256]{0,1,2:T(8,128)} async-done(((f32[384,32,256]{0,1,2:T(8,128)}), f32[384,32,256]{0,1,2:T(8,128)}, u32[]{:S(2)}, u32[]{:S(2)}) %all-to-all-start.3) | async-done | bytes 12582944 | tf_op jit(solution)/shard_map/all_to_all | solution.py:31
  1821.6 16.1 copy.68
  1837.8 12.9 copy.77
  1850.7 0.0 copy-done.3
  1850.7 14.9 fusion.29
  1865.6 14.0 reshape_reshape.15
  1879.6 9.3 subtract_multiply_fusion
  1888.9 3.1 slice_bitcast_fusion
  1892.1 3.3 fusion.18
  (24 shorter events, 0.1 us)
Async XLA Ops:
  7.2 647.0 %copy-start = (f32[256,256]{1,0:T(8,128)S(1)}, f32[256,256]{1,0:T(8,128)}, u32[]{:S(2)}) copy-start(f32[256,256]{1,0:T(8,128)} %param.30) | copy-start | bytes 786436
  7.2 578.6 %all-gather.3.cloned.1.call-start = ((), (), s32[]{:S(2)}) async-start(), calls=%async_computation.4 | async-start | bytes 31457280 | tf_op jit(solution)/shard_map/all_gather | solution.py:74
  127.3 17.7 copy-start.7
  153.8 7.5 copy-start.11
  153.8 8.2 copy-start.4
  153.8 8.2 copy-start.10
  161.0 1454.9 %all-gather.5.cloned.1.call-start = ((), (), s32[]{:S(2)}) async-start(), calls=%async_computation.5 | async-start | bytes 31457280 | tf_op jit(solution)/shard_map/all_gather | solution.py:91
  585.8 17.0 copy-start.1
  945.9 21.5 %copy-start.2 = (f32[256,256]{1,0:T(8,128)S(1)}, f32[256,256]{1,0:T(8,128)}, u32[]{:S(2)}) copy-start(f32[256,256]{1,0:T(8,128)} %param.31) | copy-start | bytes 786436
  1013.7 19.9 %copy-start.9 = (f32[4,32,256]{2,1,0:T(8,128)S(1)}, f32[4,32,256]{2,1,0:T(8,128)}, u32[]{:S(2)}) copy-start(f32[4,32,256]{2,1,0:T(8,128)} %param.25) | copy-start | bytes 393220
  1025.0 8.5 copy-start.6
  1149.9 17.7 copy-start.8
  1185.1 430.8 %copy-start.12 = (f32[16,32]{1,0:T(8,128)S(1)}, f32[16,32]{1,0:T(8,128)}, u32[]{:S(2)}) copy-start(f32[16,32]{1,0:T(8,128)} %param.22) | copy-start | bytes 6148
  1194.2 456.4 %copy-start.5 = (f32[8,32,256]{2,1,0:T(8,128)S(1)}, f32[8,32,256]{2,1,0:T(8,128)}, u32[]{:S(2)}) copy-start(f32[8,32,256]{2,1,0:T(8,128)} %param.26) | copy-start | bytes 786436
  1677.2 144.4 %all-to-all-start.3 = ((f32[384,32,256]{0,1,2:T(8,128)}), f32[384,32,256]{0,1,2:T(8,128)}, u32[]{:S(2)}, u32[]{:S(2)}) async-start(f32[384,32,256]{0,1,2:T(8,128)} %copy.66), calls=%async_computation.3 | async-start | bytes 25165824 | tf_op jit(solution)/shard_map/all_to_all | solution.py:31
  1837.8 12.9 copy-start.3
  1865.6 14.0 copy-start.13
  1865.6 26.4 %slice-start = ((s8[6291456]{0:T(1024)(128)(4,1)}), s8[2097152]{0:T(1024)(128)(4,1)S(1)}, s32[]{:S(2)}) async-start(s8[6291456]{0:T(1024)(128)(4,1)} %bitcast.108), calls=%async_computation.6 | async-start | bytes 4194304
  1879.6 12.4 slice-start.1
Sparse Core Ops, SparseCore 0:
  161.1 424.5 all-gather.2
  1194.4 421.5 all-gather.4
where the time goes:
time: 1910 us; the launch traced here: 1900 us
  waiting for transfers between devices  958 us (50%)
  blocking collectives  431 us (23%)
  local copies, waits for them, and re-layouts  265 us (14%)
  matrix products  174 us (9%)
  other arithmetic  54.3 us (3%)
    all_gather x1, waiting for transfers between devices, on_device(): portion = lax.all_gather(coeffs, 'limb', axis=1, tiled=True)  423 us
    all_gather x1, waiting for transfers between devices, on_device(): lax.all_gather(special, 'limb', axis=2, tiled=True)  422 us
    all_to_all x1, blocking collectives, to_values(): lax.all_to_all(flattened, 'coef', split_axis=2, concat_axis=1, tiled=True)  234 us
    all_to_all x2, blocking collectives, columns_section(): lax.all_to_all(flattened, 'coef', split_axis=2, concat_axis=1, tiled=True)  197 us
    all_to_all x1, waiting for transfers between devices, to_values(): lax.all_to_all(flattened, 'coef', split_axis=2, concat_axis=1, tiled=True)  113 us
    all_to_all x4, local copies, waits for them, and re-layouts, to_values(): lax.all_to_all(flattened, 'coef', split_axis=2, concat_axis=1, tiled=True)  64.7 us
  transfers between devices with their start and end apart: 3, of which 3 were waited for; matrix products, arithmetic and copies ran while one was open for 1% of the time, Pallas kernels for 0%

commit v1 on v0

--- a/solution.py
+++ b/solution.py
@@ -1,3 +1,4 @@
+import functools
 import jax
 import jax.numpy as jnp
 from jax import lax
@@ -7,6 +8,14 @@
 ROWS = 256
 COLS = 256
 HIGHEST = lax.Precision.HIGHEST
+
+
+def pair_corner(t0, dim_at):
+    latest = jnp.concatenate(lax.all_gather(t0, "limb"), dim_at)
+    return latest
+
+
+rings_list = functools.partial(pair_corner, dim_at=2)
 
 
 def columns_section(values, twiddle, inverse_columns):
@@ -86,12 +95,7 @@
     special = to_coefficients(shaped_sp, inverse_special, inverse_rows, inverse_columns)
     special = special.reshape(ciphers, 2, local_special, positions)
     own_lower = lax.dynamic_slice_in_dim(lower_table, limb_index * local_main, local_main, 1)
-    lowered = jnp.einsum(
-        "bsjn,jt->bstn",
-        lax.all_gather(special, "limb", axis=2, tiled=True),
-        own_lower,
-        precision=HIGHEST,
-    )
+    lowered = jnp.einsum("bsjn,jt->bstn", rings_list(special), own_lower, precision=HIGHEST)
     lowered = to_values(
         lowered.reshape(ciphers, 2, local_main, cols_here, ROWS),
         forward_main,

time: 1910 us -> 1950 us (1.021)
  local copies, waits for them, and re-layouts: 265 us -> 324 us
    reshape x0 -> x2, local copies, waits for them, and re-layouts: none -> 58.8 us  [pair_corner(): latest = jnp.concatenate(lax.all_gather(t0, 'limb'), dim_at)]
where the time goes in v1:
time: 1950 us; the launch traced here: 1940 us
  waiting for transfers between devices  958 us (49%)
  blocking collectives  431 us (22%)
  local copies, waits for them, and re-layouts  324 us (17%)
  matrix products  157 us (8%)
  other arithmetic  54.3 us (3%)
    all_gather x1, waiting for transfers between devices, on_device(): portion = lax.all_gather(coeffs, 'limb', axis=1, tiled=True)  423 us
    all_gather x1, waiting for transfers between devices, pair_corner(): latest = jnp.concatenate(lax.all_gather(t0, 'limb'), dim_at)  422 us
    all_to_all x1, blocking collectives, to_values(): lax.all_to_all(flattened, 'coef', split_axis=2, concat_axis=1, tiled=True)  234 us
    all_to_all x2, blocking collectives, columns_section(): lax.all_to_all(flattened, 'coef', split_axis=2, concat_axis=1, tiled=True)  197 us
    all_to_all x1, waiting for transfers between devices, to_values(): lax.all_to_all(flattened, 'coef', split_axis=2, concat_axis=1, tiled=True)  113 us
    all_to_all x4, local copies, waits for them, and re-layouts, to_values(): lax.all_to_all(flattened, 'coef', split_axis=2, concat_axis=1, tiled=True)  64.7 us
    reshape x2, local copies, waits for them, and re-layouts, pair_corner(): latest = jnp.concatenate(lax.all_gather(t0, 'limb'), dim_at)  58.8 us
  transfers between devices with their start and end apart: 3, of which 3 were waited for; matrix products, arithmetic and copies ran while one was open for 1% of the time, Pallas kernels for 0%

profile of v1, /device:TPU:0, one launch (start us, length us, event | category | flops | bytes accessed | tf_op | source)
XLA Modules:
  0.0 1944.1 jit_solution(12884193095064419766)
XLA Ops:
  7.2 0.0 copy-start
  7.2 0.0 all-gather.3.cloned.1.call-start
  7.2 10.8 broadcast_multiply_fusion.3
  18.0 9.6 copy.50
  27.6 99.4 %all_to_all.72 = f32[192,32,256]{0,1,2:T(8,128)S(1)} all-to-all(f32[192,32,256]{0,1,2:T(8,128)} %copy.50), channel_id=1, replica_groups=mesh['limb'=4,'coef'=8] {'coef'}, dimensions={2} | all-to-all | bytes 12582912 | tf_op jit(solution)/shard_map/all_to_all | solution.py:26
  126.9 8.0 copy.52
  134.9 9.7 copy.53
  144.6 0.0 copy-done.7
  144.6 8.8 fusion.33
  153.5 7.2 reshape_reshape.9
  160.7 0.0 all-gather.3.cloned.1.call-update
  160.7 0.3 all-gather.5.cloned.1.call-start
  161.0 0.0 copy-done.11
  161.0 0.1 copy.48
  161.0 0.7 constant_dynamic-slice_fusion
  161.7 0.0 copy-done.4
  161.7 0.0 copy-done.10
  161.8 0.6 compare_convert_fusion
  162.3 423.1 %all-gather.3.cloned.1.call-done = f32[24,32,8192]{2,1,0:T(8,128)} async-done(((f32[24,8,8192]{2,1,0:T(8,128)}), f32[24,32,8192]{2,1,0:T(8,128)}) %all-gather.3.cloned.1.call-update) | async-done | bytes 25165840 | tf_op jit(solution)/shard_map/all_gather | solution.py:83
  585.4 16.9 fusion.11
  602.4 0.0 copy-done.1
  602.4 15.7 fusion.8
  618.1 14.2 pad_maximum_fusion
  632.3 21.5 %reshape.95 = f32[24,2,12,32,256]{4,3,2,0,1:T(8,128)} reshape(f32[24,2,12,8192]{3,2,0,1:T(8,128)} %pad_maximum_fusion) | data formatting | bytes 37748736 | tf_op jit(solution)/shard_map/reshape | solution.py:87
  653.8 0.0 copy-done
  653.8 20.6 %broadcast_multiply_fusion = f32[24,2,12,32,256]{4,3,2,1,0:T(8,128)} fusion(f32[12,32,256]{2,1,0:T(8,128)S(1)} %pad_maximum_fusion.1, f32[24,2,12,32,256]{4,3,2,0,1:T(8,128)} %reshape.95, f32[256,256]{1,0:T(8,128)S(1)} %copy-done), kind=kOutput, calls=%fused_computation.14 | convolution fusion | flops 14500233216 | bytes 38404096 | tf_op jit(solution)/shard_map/...cr,rk->...ck/dot_general | solution.py:38
  674.5 23.4 %copy.56 = f32[576,32,256]{0,1,2:T(8,128)} copy(f32[576,32,256]{2,1,0:T(8,128)} %bitcast.98) | data formatting | bytes 37748736 | tf_op jit(solution)/shard_map/reshape | solution.py:39
  697.9 233.6 %all_to_all.73 = f32[576,32,256]{0,1,2:T(8,128)S(1)} all-to-all(f32[576,32,256]{0,1,2:T(8,128)} %copy.56), channel_id=1, replica_groups=mesh['limb'=4,'coef'=8] {'coef'}, dimensions={2} | all-to-all | bytes 37748736 | tf_op jit(solution)/shard_map/all_to_all | solution.py:40
  931.5 14.1 copy.58
  945.6 21.5 %copy.59 = f32[576,256,32]{1,2,0:T(8,128)} copy(f32[576,256,32]{0,2,1:T(8,128)} %bitcast.100) | data formatting | bytes 37748736 | tf_op jit(solution)/shard_map/all_to_all | solution.py:40
  967.1 0.0 copy-done.2
  967.1 20.2 %fusion.29 = f32[576,32,256]{2,1,0:T(8,128)} fusion(f32[576,256,32]{1,2,0:T(8,128)} %copy.59, f32[256,256]{1,0:T(8,128)S(1)} %copy-done.2), kind=kOutput, calls=%fused_computation.30 | convolution fusion | flops 14495514624 | bytes 38010880 | tf_op jit(solution)/shard_map/bck,cm->bkm/dot_general | solution.py:41
  987.3 20.6 %reshape_reshape.10 = f32[24,2,12,8192]{3,2,1,0:T(8,128)} reshape(f32[576,32,256]{2,1,0:T(8,128)} %fusion.29) | data formatting | bytes 37748736 | tf_op jit(solution)/shard_map/reshape;reshape | solution.py:89
  1007.8 5.5 slice.17
  1013.4 0.0 copy-start.9
  1013.4 11.3 multiply_reduce_fusion.1
  1024.7 8.5 reshape.80
  1033.2 9.1 broadcast_multiply_fusion.2
  1042.3 9.6 copy.61
  1051.9 97.8 %all_to_all.74 = f32[192,32,256]{0,1,2:T(8,128)S(1)} all-to-all(f32[192,32,256]{0,1,2:T(8,128)} %copy.61), channel_id=1, replica_groups=mesh['limb'=4,'coef'=8] {'coef'}, dimensions={2} | all-to-all | bytes 12582912 | tf_op jit(solution)/shard_map/all_to_all | solution.py:26
  1149.6 8.0 copy.63
  1157.6 9.7 copy.64
  1167.3 8.8 fusion.31
  1176.2 8.6 all_gather_reshape_reshape.3
  1184.8 9.1 copy.65
  1193.9 0.0 all-gather.5.cloned.1.call-update
  1193.9 421.7 %all-gather.5.cloned.1.call-done = f32[4,24,2,4,8192]{4,1,3,2,0:T(8,128)} async-done(((f32[1,24,2,4,8192]{4,1,3,2,0:T(8,128)}), f32[4,24,2,4,8192]{4,1,3,2,0:T(8,128)}) %all-gather.5.cloned.1.call-update) | async-done | bytes 25165840 | tf_op jit(solution)/shard_map/all_gather | solution.py:14
  1615.6 30.0 %copy.66 = f32[24,2,4,4,8192]{4,3,2,1,0:T(4,128)} copy(f32[24,2,4,4,8192]{4,0,3,1,2:T(8,128)} %bitcast.108) | data formatting | bytes 50331648 | tf_op jit(solution)/shard_map/reshape | solution.py:14
  1645.6 28.8 %reshape.83 = f32[24,2,16,8192]{3,2,1,0:T(8,128)} reshape(f32[24,2,4,4,8192]{4,3,2,1,0:T(4,128)} %copy.66) | data formatting | bytes 50331648 | tf_op jit(solution)/shard_map/reshape | solution.py:14
  1674.5 17.3 fusion.35
  1691.7 14.1 broadcast_multiply_fusion.1
  1705.8 12.9 copy.68
  1718.7 5.6 all-to-all-start.3
  1724.3 10.4 slice.16
  1734.7 15.5 multiply_reduce_fusion
  1750.2 113.0 %all-to-all-done.3 = f32[384,32,256]{0,1,2:T(8,128)} async-done(((f32[384,32,256]{0,1,2:T(8,128)}), f32[384,32,256]{0,1,2:T(8,128)}, u32[]{:S(2)}, u32[]{:S(2)}) %all-to-all-start.3) | async-done | bytes 12582944 | tf_op jit(solution)/shard_map/all_to_all | solution.py:40
  1863.2 16.1 copy.70
  1879.4 12.9 copy.79
  1892.3 14.9 fusion.27
  1907.3 14.0 reshape_reshape.11
  1921.3 9.3 subtract_multiply_fusion
  1930.6 3.1 slice_bitcast_fusion
  1933.7 0.0 slice-done
  1933.7 3.3 fusion.16
  (26 shorter events, 0.1 us)
Async XLA Ops:
  7.2 646.7 %copy-start = (f32[256,256]{1,0:T(8,128)S(1)}, f32[256,256]{1,0:T(8,128)}, u32[]{:S(2)}) copy-start(f32[256,256]{1,0:T(8,128)} %param.30) | copy-start | bytes 786436
  7.2 578.2 %all-gather.3.cloned.1.call-start = ((), (), s32[]{:S(2)}) async-start(), calls=%async_computation.4 | async-start | bytes 31457280 | tf_op jit(solution)/shard_map/all_gather | solution.py:83
  126.9 17.7 copy-start.7
  153.4 7.5 copy-start.11
  153.5 8.3 copy-start.4
  153.5 8.3 copy-start.10
  160.7 1454.9 %all-gather.5.cloned.1.call-start = ((), (), s32[]{:S(2)}) async-start(), calls=%async_computation.5 | async-start | bytes 31457280 | tf_op jit(solution)/shard_map/all_gather | solution.py:14
  585.4 17.0 copy-start.1
  945.6 21.5 %copy-start.2 = (f32[256,256]{1,0:T(8,128)S(1)}, f32[256,256]{1,0:T(8,128)}, u32[]{:S(2)}) copy-start(f32[256,256]{1,0:T(8,128)} %param.31) | copy-start | bytes 786436
  1013.4 19.9 %copy-start.9 = (f32[4,32,256]{2,1,0:T(8,128)S(1)}, f32[4,32,256]{2,1,0:T(8,128)}, u32[]{:S(2)}) copy-start(f32[4,32,256]{2,1,0:T(8,128)} %param.25) | copy-start | bytes 393220
  1024.7 8.5 copy-start.6
  1149.6 17.7 copy-start.8
  1645.6 28.8 %copy-start.12 = (f32[16,32]{1,0:T(8,128)S(1)}, f32[16,32]{1,0:T(8,128)}, u32[]{:S(2)}) copy-start(f32[16,32]{1,0:T(8,128)} %param.22) | copy-start | bytes 6148
  1674.5 17.3 copy-start.5
  1718.7 144.6 %all-to-all-start.3 = ((f32[384,32,256]{0,1,2:T(8,128)}), f32[384,32,256]{0,1,2:T(8,128)}, u32[]{:S(2)}, u32[]{:S(2)}) async-start(f32[384,32,256]{0,1,2:T(8,128)} %copy.68), calls=%async_computation.3 | async-start | bytes 25165824 | tf_op jit(solution)/shard_map/all_to_all | solution.py:40
  1879.4 12.9 copy-start.3
  1907.3 14.0 copy-start.13
  1907.3 26.4 %slice-start = ((s8[6291456]{0:T(1024)(128)(4,1)}), s8[2097152]{0:T(1024)(128)(4,1)S(1)}, s32[]{:S(2)}) async-start(s8[6291456]{0:T(1024)(128)(4,1)} %bitcast.112), calls=%async_computation.6 | async-start | bytes 4194304
  1921.3 12.4 slice-start.1
Sparse Core Ops, SparseCore 0:
  160.8 424.5 all-gather.2
  1194.1 421.4 all-gather.4
